TPU v7x, 32 devices: a whole 2x2x4 slice. The times are simulated.
32 devices in a mesh: dom: 8 (over y, x, core), dim: 4 (over z).
Axes of the slice: x: 2, y: 2, z: 4, core: 2. Of those that a mesh axis runs over, the one named last changes fastest.
Arguments:
- particles: float32 [64, 1024], P('dom', 'dim'), may hold values from -5 to 5
- data_rows: bfloat16 [64, 16, 1024], P('dom', None, 'dim'), may hold values from -0.375 to 0.375
- labels: int32 [64, 16], P('dom'), may hold values from 0 to 1
Outputs:
- updates: float32 [2, 64, 1024], P(None, 'dom', 'dim')
All inputs are finite; a program needn't handle non-finite values.
Results may differ from a plain program's by a relative error of at most 0.0003.
Values may be sent and summed in bfloat16 or wider, within the bound.
A program may use at most 64 MiB of HBM per device.

v0:
```python
from functools import partial

import jax
import jax.numpy as jnp
from jax import lax
from jax.sharding import PartitionSpec as P

NEWTON = 2
CG_STEPS = 2
BAND = 1


prior_precision = 0.05
like_weight = 4.0
move_size = 0.5
highest = lax.Precision.HIGHEST


def drift_terms(x_local, squares, kernel_scale, rows_pos, rows_grad):
    inner_rows = jnp.einsum("id,jd->ij", x_local, rows_pos, precision=highest)
    row_squares = jnp.sum(rows_pos * rows_pos, axis=1)
    distance = squares[:, None] + row_squares[None, :] - 2.0 * inner_rows
    kernel = jnp.exp(-distance / kernel_scale)
    kernel_sq = kernel * kernel
    kernel_grad = jnp.dot(kernel, rows_grad, precision=highest)
    kernel_pos = jnp.dot(kernel, rows_pos, precision=highest)
    square_pos = jnp.dot(kernel_sq, rows_pos, precision=highest)
    return (
        kernel,
        kernel_grad,
        kernel_pos,
        square_pos,
        jnp.sum(kernel, axis=1),
        jnp.sum(kernel_sq, axis=1),
    )


def pair_block(running, piece, start, kernel, curve_rows, pos_rows, vectors, cross_scale):
    weight_sq = (kernel * kernel).T
    factor_part = piece.astype(jnp.float32)
    projected = jnp.einsum("jrd,id->jri", factor_part, vectors, precision=highest)
    weighted = projected * curve_rows[:, :, None] * weight_sq[:, None, :]
    running = jnp.einsum("jrd,jri->id", factor_part, weighted, precision=highest)
    along_pair = jnp.einsum("jd,id->ji", pos_rows, vectors, precision=highest)
    return running + cross_scale * jnp.einsum(
        "ji,jd->id", weight_sq * along_pair, pos_rows, precision=highest
    )


def residual_sum(vectors):
    return lax.psum(jnp.sum(vectors * vectors), ("dom", "dim"))


def per_device(particles, data_rows, labels):
    dim_count = lax.axis_size("dim")
    dom_count = lax.axis_size("dom")
    part_rows = particles.shape[0]
    slice_width = particles.shape[1]
    width = slice_width * dim_count
    quarter = part_rows // dim_count
    total_count = part_rows * dom_count
    kernel_scale = 1.0 * BAND * width
    cross_scale = 4.0 / (kernel_scale * kernel_scale)
    lane = lax.axis_index("dim")
    first_row = lane * quarter
    first_col = lane * slice_width
    own_factors = lax.all_to_all(data_rows, "dim", split_axis=0, concat_axis=2, tiled=True)
    factor_float = own_factors.astype(jnp.float32)
    own_targets = lax.dynamic_slice_in_dim(labels, first_row, quarter, 0).astype(jnp.float32)
    current = particles
    outputs = []
    for newton_step in range(NEWTON):
        x_local = lax.all_gather(current, "dim", axis=1, tiled=True)
        own_pos = lax.dynamic_slice_in_dim(x_local, first_row, quarter, 0)
        logits = jnp.einsum("jrd,jd->jr", factor_float, own_pos, precision=highest)
        probs = jax.nn.sigmoid(logits)
        own_grad = -prior_precision * own_pos + like_weight * jnp.einsum(
            "jr,jrd->jd", own_targets - probs, factor_float, precision=highest
        )
        own_curve = like_weight * probs * (1.0 - probs)
        pos_rows, grad_rows, curve_rows = (
            lax.all_gather(own_pos, "dom", axis=0, tiled=True),
            lax.all_gather(own_grad, "dom", axis=0, tiled=True),
            lax.all_gather(own_curve, "dom", axis=0, tiled=True),
        )
        squares = jnp.sum(x_local * x_local, axis=1)
        kernel, kernel_grad, kernel_pos, square_pos, kernel_total, square_total = drift_terms(
            x_local, squares, kernel_scale, pos_rows, grad_rows
        )
        kernel_grad, kernel_pos, square_pos, kernel_total, square_total = lax.psum(
            (kernel_grad, kernel_pos, square_pos, kernel_total, square_total), "dim"
        )
        drift_full = (
            kernel_grad + 2.0 / kernel_scale * (x_local * kernel_total[:, None] - kernel_pos)
        ) / total_count
        drift = lax.dynamic_slice_in_dim(drift_full, first_col, slice_width, 1)
        mean_slice = lax.dynamic_slice_in_dim(square_pos, first_col, slice_width, 1)
        solution = jnp.zeros_like(drift)
        residual = drift
        direction = drift
        norm_now = residual_sum(residual)
        for solve_step in range(CG_STEPS):
            vectors_full = lax.all_gather(direction, "dim", axis=1, tiled=True)
            start_total = jnp.zeros((part_rows, width), jnp.float32)
            block_step = partial(
                pair_block,
                kernel=kernel,
                curve_rows=curve_rows,
                pos_rows=pos_rows,
                vectors=vectors_full,
                cross_scale=cross_scale,
            )
            pairs = block_step(
                start_total, lax.all_gather(own_factors, "dom", axis=0, tiled=True), jnp.int32(0)
            )
            pairs = lax.psum_scatter(pairs, "dim", scatter_dimension=1, tiled=True)
            along_self = jnp.sum(x_local * vectors_full, axis=1)
            along_mean = jnp.sum(vectors_full * square_pos, axis=1)
            local = prior_precision * square_total[:, None] * direction + cross_scale * (
                current * (along_self * square_total - along_mean)[:, None]
                - along_self[:, None] * mean_slice
            )
            image = (pairs + local) / total_count
            curve_total, mixed_total, image_square = lax.psum(
                (jnp.sum(direction * image), jnp.sum(residual * image), jnp.sum(image * image)),
                ("dom", "dim"),
            )
            alpha = norm_now / curve_total
            norm_next = norm_now - 2.0 * alpha * mixed_total + alpha * alpha * image_square
            solution = solution + alpha * direction
            residual = residual - alpha * image
            if solve_step + 1 < CG_STEPS:
                direction = residual + norm_next / norm_now * direction
                norm_now = norm_next
        outputs.append(solution)
        current = current + move_size * solution
    return jnp.stack(outputs)


def solution(mesh):
    placed = (P("dom", "dim"), P("dom", None, "dim"), P("dom", None))
    return jax.shard_map(
        per_device, mesh=mesh, in_specs=placed, out_specs=P(None, "dom", "dim"), check_vma=False
    )
```

profile of v0, /device:TPU:0, one launch (start us, length us, event | category | flops | bytes accessed | tf_op | source)
XLA Modules:
  0.0 489.6 jit_solution(9462814069500571010)
XLA Ops:
  6.5 6.3 %all-to-all-start = ((bf16[8,16,256]{2,1,0:T(8,128)(2,1)}), bf16[8,16,256]{2,1,0:T(8,128)(2,1)S(1)}, u32[]{:S(2)}, u32[]{:S(2)}) async-start(bf16[8,16,256]{2,1,0:T(8,128)(2,1)} %param.4), calls=%async_computation | async-start | bytes 131072 | tf_op jit(solution)/shard_map/all_to_all | solution.py:67
  13.6 13.7 %all_gather.42 = f32[8,1024]{1,0:T(8,128)S(1)} all-gather(f32[8,256]{1,0:T(8,128)S(1)} %copy-done.2), channel_id=1, replica_groups=mesh['dom'=8,'dim'=4] {'dim'}, dimensions={1}, use_global_device_ids=true | all-gather | bytes 40960 | tf_op jit(solution)/shard_map/all_gather | solution.py:73
  28.6 9.3 %all-gather = f32[8,2,1024]{2,1,0:T(2,128)S(1)} all-gather(f32[1,2,1024]{2,1,0:T(2,128)S(1)} %get-tuple-element.47), channel_id=1, replica_groups=mesh['dom'=8,'dim'=4] {'dom'}, dimensions={0}, use_global_device_ids=true | all-gather | bytes 73728 | tf_op jit(solution)/shard_map/all_gather | solution.py:82
  40.6 9.2 %all-gather.1 = f32[8,2,1024]{2,1,0:T(2,128)S(1)} all-gather(f32[1,2,1024]{2,1,0:T(2,128)S(1)} %get-tuple-element.48), channel_id=1, replica_groups=mesh['dom'=8,'dim'=4] {'dom'}, dimensions={0}, use_global_device_ids=true | all-gather | bytes 73728 | tf_op jit(solution)/shard_map/all_gather | solution.py:83
  50.8 7.9 %all-gather.2 = f32[8,2,16]{2,1,0:T(2,128)S(1)} all-gather(f32[1,2,16]{2,1,0:T(2,128)S(1)} %get-tuple-element.43), channel_id=1, replica_groups=mesh['dom'=8,'dim'=4] {'dom'}, dimensions={0}, use_global_device_ids=true | all-gather | bytes 1152 | tf_op jit(solution)/shard_map/all_gather | solution.py:84
  58.8 9.8 %all_gather.46 = bf16[16,16,1024]{2,1,0:T(8,128)(2,1)S(1)} all-gather(bf16[2,16,1024]{2,1,0:T(8,128)(2,1)S(1)} %all_to_all.16), channel_id=1, replica_groups=mesh['dom'=8,'dim'=4] {'dom'}, dimensions={0}, use_global_device_ids=true | all-gather | bytes 589824 | tf_op jit(solution)/shard_map/all_gather | solution.py:114
  68.6 25.0 %all-reduce.9.cloned.1.call-done = (f32[8,1024]{1,0:T(8,128)}, f32[8,1024]{1,0:T(8,128)}, f32[8]{0:T(128)}, f32[8,1024]{1,0:T(8,128)}, f32[8]{0:T(128)}) async-done(((f32[8,1024]{1,0:T(8,128)}, f32[8,1024]{1,0:T(8,128)}, f32[8]{0:T(128)}, f32[8,1024]{1,0:T(8,128)}, f32[8]{0:T(128)}), (f32[8,1024]{1,0:T(8,128)}, f32[8,1024]{1,0:T(8,128)}, f32[8]{0:T(128)}, f32[8,1024]{1,0:T(8,128)}, ...) | async-done | bytes 98384 | tf_op jit(solution)/shard_map/psum | solution.py:90
  95.0 13.2 %all_gather.45 = f32[8,1024]{1,0:T(8,128)S(1)} all-gather(f32[8,256]{1,0:T(8,128)S(1)} %fusion.18), channel_id=1, replica_groups=mesh['dom'=8,'dim'=4] {'dim'}, dimensions={1}, use_global_device_ids=true | all-gather | bytes 40960 | tf_op jit(solution)/shard_map/all_gather | solution.py:103
  109.1 1.9 fusion.4
  113.3 18.7 %reduce-scatter.5.cloned.1.call-done = f32[8,256]{1,0:T(8,128)} async-done(((f32[8,1024]{1,0:T(8,128)}), f32[8,256]{1,0:T(8,128)}) %reduce-scatter.5.cloned.1.call-update) | async-done | bytes 8208 | tf_op jit(solution)/shard_map/reduce_scatter | solution.py:116
  132.0 1.5 multiply_reduce_fusion.17
  133.4 38.7 %all-reduce.1 = (f32[]{:T(128)}, f32[]{:T(128)}, f32[]{:T(128)}) all-reduce(f32[]{:T(128)} %get-tuple-element.18, f32[]{:T(128)} %get-tuple-element.17, f32[]{:T(128)} %get-tuple-element.16), channel_id=1, replica_groups=mesh['dom'=8,'dim'=4] {'dom','dim'}, use_global_device_ids=true, to_apply=%region_7.0 | all-reduce | flops 3 | bytes 24 | tf_op jit(solution)/shard_map/psum | solution.py:51
  176.0 13.1 %all_gather.48 = f32[8,1024]{1,0:T(8,128)S(1)} all-gather(f32[8,256]{1,0:T(8,128)S(1)} %multiply_add_fusion.3), channel_id=1, replica_groups=mesh['dom'=8,'dim'=4] {'dim'}, dimensions={1}, use_global_device_ids=true | all-gather | bytes 40960 | tf_op jit(solution)/shard_map/all_gather | solution.py:103
  189.5 2.0 fusion.5
  193.0 19.3 %reduce-scatter.7.cloned.1.call-done = f32[8,256]{1,0:T(8,128)} async-done(((f32[8,1024]{1,0:T(8,128)}), f32[8,256]{1,0:T(8,128)}) %reduce-scatter.7.cloned.1.call-update) | async-done | bytes 8208 | tf_op jit(solution)/shard_map/reduce_scatter | solution.py:116
  212.3 1.4 multiply_reduce_fusion.16
  213.7 38.6 %psum.140 = f32[]{:T(128)} all-reduce(f32[]{:T(128)} %multiply_reduce_fusion.16), channel_id=1, replica_groups=mesh['dom'=8,'dim'=4] {'dom','dim'}, use_global_device_ids=true, to_apply=%region_22.0 | all-reduce | flops 1 | bytes 8 | tf_op jit(solution)/shard_map/psum | solution.py:124
  253.0 13.1 %all_gather.49 = f32[8,1024]{1,0:T(8,128)S(1)} all-gather(f32[8,256]{1,0:T(8,128)S(1)} %get-tuple-element.50), channel_id=1, replica_groups=mesh['dom'=8,'dim'=4] {'dim'}, dimensions={1}, use_global_device_ids=true | all-gather | bytes 40960 | tf_op jit(solution)/shard_map/all_gather | solution.py:73
  266.7 10.2 %all-gather.3 = f32[8,2,1024]{2,1,0:T(2,128)S(1)} all-gather(f32[1,2,1024]{2,1,0:T(2,128)S(1)} %get-tuple-element.45), channel_id=1, replica_groups=mesh['dom'=8,'dim'=4] {'dom'}, dimensions={0}, use_global_device_ids=true | all-gather | bytes 73728 | tf_op jit(solution)/shard_map/all_gather | solution.py:82
  279.6 8.4 %all-gather.4 = f32[8,2,1024]{2,1,0:T(2,128)S(1)} all-gather(f32[1,2,1024]{2,1,0:T(2,128)S(1)} %get-tuple-element.46), channel_id=1, replica_groups=mesh['dom'=8,'dim'=4] {'dom'}, dimensions={0}, use_global_device_ids=true | all-gather | bytes 73728 | tf_op jit(solution)/shard_map/all_gather | solution.py:83
  289.0 8.8 %all-gather.5 = f32[8,2,16]{2,1,0:T(2,128)S(1)} all-gather(f32[1,2,16]{2,1,0:T(2,128)S(1)} %get-tuple-element.40), channel_id=1, replica_groups=mesh['dom'=8,'dim'=4] {'dom'}, dimensions={0}, use_global_device_ids=true | all-gather | bytes 1152 | tf_op jit(solution)/shard_map/all_gather | solution.py:84
  297.8 24.8 %all-reduce.7.cloned.1.call-done = (f32[8,1024]{1,0:T(8,128)}, f32[8,1024]{1,0:T(8,128)}, f32[8]{0:T(128)}, f32[8,1024]{1,0:T(8,128)}, f32[8]{0:T(128)}) async-done(((f32[8,1024]{1,0:T(8,128)}, f32[8,1024]{1,0:T(8,128)}, f32[8]{0:T(128)}, f32[8,1024]{1,0:T(8,128)}, f32[8]{0:T(128)}), (f32[8,1024]{1,0:T(8,128)}, f32[8,1024]{1,0:T(8,128)}, f32[8]{0:T(128)}, f32[8,1024]{1,0:T(8,128)}, ...) | async-done | bytes 98384 | tf_op jit(solution)/shard_map/psum | solution.py:90
  324.1 13.4 %all_gather.52 = f32[8,1024]{1,0:T(8,128)S(1)} all-gather(f32[8,256]{1,0:T(8,128)S(1)} %fusion.16), channel_id=1, replica_groups=mesh['dom'=8,'dim'=4] {'dim'}, dimensions={1}, use_global_device_ids=true | all-gather | bytes 40960 | tf_op jit(solution)/shard_map/all_gather | solution.py:103
  338.4 1.9 fusion.6
  342.5 18.7 %reduce-scatter.9.cloned.1.call-done = f32[8,256]{1,0:T(8,128)} async-done(((f32[8,1024]{1,0:T(8,128)}), f32[8,256]{1,0:T(8,128)}) %reduce-scatter.9.cloned.1.call-update) | async-done | bytes 8208 | tf_op jit(solution)/shard_map/reduce_scatter | solution.py:116
  361.2 1.5 multiply_reduce_fusion.13
  362.6 38.6 %all-reduce = (f32[]{:T(128)}, f32[]{:T(128)}, f32[]{:T(128)}) all-reduce(f32[]{:T(128)} %get-tuple-element.15, f32[]{:T(128)} %get-tuple-element.14, f32[]{:T(128)} %get-tuple-element.13), channel_id=1, replica_groups=mesh['dom'=8,'dim'=4] {'dom','dim'}, use_global_device_ids=true, to_apply=%region_30.0 | all-reduce | flops 3 | bytes 24 | tf_op jit(solution)/shard_map/psum | solution.py:51
  405.2 13.2 %all_gather.54 = f32[8,1024]{1,0:T(8,128)S(1)} all-gather(f32[8,256]{1,0:T(8,128)S(1)} %multiply_add_fusion), channel_id=1, replica_groups=mesh['dom'=8,'dim'=4] {'dim'}, dimensions={1}, use_global_device_ids=true | all-gather | bytes 40960 | tf_op jit(solution)/shard_map/all_gather | solution.py:103
  418.7 2.0 fusion.7
  422.2 19.4 %reduce-scatter.11.cloned.1.call-done = f32[8,256]{1,0:T(8,128)} async-done(((f32[8,1024]{1,0:T(8,128)}), f32[8,256]{1,0:T(8,128)}) %reduce-scatter.11.cloned.1.call-update) | async-done | bytes 8208 | tf_op jit(solution)/shard_map/reduce_scatter | solution.py:116
  441.5 1.4 multiply_reduce_fusion.12
  442.9 38.6 %psum.149 = f32[]{:T(128)} all-reduce(f32[]{:T(128)} %multiply_reduce_fusion.12), channel_id=1, replica_groups=mesh['dom'=8,'dim'=4] {'dom','dim'}, use_global_device_ids=true, to_apply=%region_45.0 | all-reduce | flops 1 | bytes 8 | tf_op jit(solution)/shard_map/psum | solution.py:124
  (90 shorter events, 23.3 us)
Async XLA Ops:
  6.5 20.9 %all-to-all-start = ((bf16[8,16,256]{2,1,0:T(8,128)(2,1)}), bf16[8,16,256]{2,1,0:T(8,128)(2,1)S(1)}, u32[]{:S(2)}, u32[]{:S(2)}) async-start(bf16[8,16,256]{2,1,0:T(8,128)(2,1)} %param.4), calls=%async_computation | async-start | bytes 131072 | tf_op jit(solution)/shard_map/all_to_all | solution.py:67
  12.9 0.7 copy-start.2
  12.9 80.7 %all-reduce.9.cloned.1.call-start = ((), (), s32[]{:S(2)}) async-start(), calls=%async_computation.10 | async-start | bytes 198656 | tf_op jit(solution)/shard_map/psum | solution.py:90
  27.7 0.7 copy-start.5
  58.7 73.2 %reduce-scatter.5.cloned.1.call-start = ((), (), s32[]{:S(2)}) async-start(), calls=%async_computation.5 | async-start | bytes 40960 | tf_op jit(solution)/shard_map/reduce_scatter | solution.py:116
  93.6 0.6 copy-start.7
  108.2 0.8 copy-start.1
  112.6 99.8 %reduce-scatter.7.cloned.1.call-start = ((), (), s32[]{:S(2)}) async-start(), calls=%async_computation.6 | async-start | bytes 40960 | tf_op jit(solution)/shard_map/reduce_scatter | solution.py:116
  112.6 0.7 copy-start.4
  192.9 129.7 %all-reduce.7.cloned.1.call-start = ((), (), s32[]{:S(2)}) async-start(), calls=%async_computation.9 | async-start | bytes 198656 | tf_op jit(solution)/shard_map/psum | solution.py:90
  288.8 72.3 %reduce-scatter.9.cloned.1.call-start = ((), (), s32[]{:S(2)}) async-start(), calls=%async_computation.7 | async-start | bytes 40960 | tf_op jit(solution)/shard_map/reduce_scatter | solution.py:116
  322.7 0.6 copy-start.6
  337.5 0.8 copy-start
  341.8 99.7 %reduce-scatter.11.cloned.1.call-start = ((), (), s32[]{:S(2)}) async-start(), calls=%async_computation.8 | async-start | bytes 40960 | tf_op jit(solution)/shard_map/reduce_scatter | solution.py:116
  341.8 0.7 copy-start.3
Sparse Core Ops, SparseCore 0:
  58.9 34.7 all-reduce.8
  112.7 19.2 reduce-scatter.4
  193.1 19.2 reduce-scatter.6
  289.0 33.6 all-reduce.6
  341.9 19.2 reduce-scatter.8
  422.3 19.2 reduce-scatter.10
where the time goes:
time: 492 us; the launch traced here: 490 us
  blocking collectives  298 us (61%)
  waiting for transfers between devices  126 us (26%)
  between operations  22.8 us (5%)
  matrix products  21.8 us (4%)
  other arithmetic  9.23 us (2%)
  starting transfers between devices  6.56 us (1%)
  local copies, waits for them, and re-layouts  5.49 us (1%)
    psum x2, blocking collectives, residual_sum(): return lax.psum(jnp.sum(vectors * vectors), ('dom', 'dim'))  77.3 us
    psum x2, blocking collectives, per_device(): lax.psum((jnp.sum(direction * image), jnp.sum(residual * image), jnp.sum(...  77.1 us
    reduce_scatter x4, waiting for transfers between devices, per_device(): pairs = lax.psum_scatter(pairs, 'dim', scatter_dimension=1, tiled=True)  76 us
    all_gather x4, blocking collectives, per_device(): vectors_full = lax.all_gather(direction, 'dim', axis=1, tiled=True)  52.9 us
    psum x2, waiting for transfers between devices, per_device(): lax.psum((kernel_grad, kernel_pos, square_pos, kernel_total, square_total...  49.8 us
    all_gather x2, blocking collectives, per_device(): x_local = lax.all_gather(current, 'dim', axis=1, tiled=True)  26.8 us
    all_gather x2, blocking collectives, per_device(): lax.all_gather(own_pos, 'dom', axis=0, tiled=True)  19.5 us
    all_gather x2, blocking collectives, per_device(): lax.all_gather(own_grad, 'dom', axis=0, tiled=True)  17.6 us
  transfers between devices with their start and end apart: 7, of which 6 were waited for; matrix products, arithmetic and copies ran while one was open for 0% of the time, Pallas kernels for 0%

commit v1 on v0

v1 whole, which is shorter than its diff:
```python
import functools

import jax
import jax.numpy as jnp
from jax import lax
from jax.experimental import pallas as pl
from jax.experimental.pallas import tpu as pltpu
from jax.sharding import PartitionSpec as P

NEWTON = 2
BAND = 1
LANES = 128

prior_precision = 0.05
like_weight = 4.0
move_size = 0.5
MESH = pl.DeviceIdType.MESH
f32 = jnp.float32
bf16 = jnp.bfloat16


def halves(v):
    high = v.astype(bf16).astype(f32)
    return jnp.concatenate([high, v - high], axis=0).astype(bf16)


def fold(product):
    rows = product.shape[0] // 2
    return product[:rows] + product[rows:]


def dot(a, b):
    return lax.dot_general(a, b, (((1,), (0,)), ((), ())), preferred_element_type=f32)


def dot_t(a, b):
    return lax.dot_general(a, b, (((1,), (1,)), ((), ())), preferred_element_type=f32)


def steps(
    nd, nz, x_ref, a_ref, y_ref, out_ref,
    basis, spread, xbuf, dist, lgt, proj, sums,
    a_send, a_recv, x_send, x_recv, d_send, d_recv, l_send, l_recv, p_send, p_recv, s_send, s_recv,
):
    rows, width = x_ref.shape
    draws = a_ref.shape[0]
    per_row = draws // rows
    count = nd * rows
    wide = dist.shape[-1]
    cols = nd * draws
    scale = 1.0 * BAND * width * nz
    cross = 4.0 / (scale * scale)
    me_dom = lax.axis_index("dom")
    me_dim = lax.axis_index("dim")
    dom_to = [None] + [lax.rem(me_dom + k, nd) for k in range(1, nd)]
    dim_to = [None] + [lax.rem(me_dim + k, nz) for k in range(1, nz)]

    def send_all(axis, src, dst, send, recv):
        to = dom_to if axis == "dom" else dim_to
        copies = []
        for k in range(1, len(to)):
            copy = pltpu.make_async_remote_copy(
                src_ref=src, dst_ref=dst(k), send_sem=send(k), recv_sem=recv(k),
                device_id={axis: to[k]}, device_id_type=MESH,
            )
            copy.start()
            copies.append(copy)
        return copies

    barrier = pltpu.get_barrier_semaphore()
    for k in range(1, nd):
        pl.semaphore_signal(barrier, inc=1, device_id={"dom": dom_to[k]}, device_id_type=MESH)
    for k in range(1, nz):
        pl.semaphore_signal(barrier, inc=1, device_id={"dim": dim_to[k]}, device_id_type=MESH)

    lane_of = lax.broadcasted_iota(jnp.int32, (rows, draws), 1) // per_row
    row_of = lax.broadcasted_iota(jnp.int32, (rows, draws), 0)
    own_block = lane_of == row_of

    def flat(values):
        return jnp.sum(jnp.where(own_block, values, 0.0), axis=0, keepdims=True)

    basis[0:draws, :] = a_ref[...]
    tile = lax.broadcasted_iota(jnp.int32, (per_row, draws), 1) % per_row
    tile = (tile == lax.broadcasted_iota(jnp.int32, (per_row, draws), 0)).astype(f32).astype(bf16)
    labels = flat(dot(y_ref[...].astype(f32).astype(bf16), tile))
    current = x_ref[...]
    pending = []
    a_copies = []
    first_eight = lax.broadcasted_iota(jnp.int32, (rows, wide), 1)
    own_pair = first_eight == lax.broadcasted_iota(jnp.int32, (rows, wide), 0)
    lane = lax.broadcasted_iota(jnp.int32, (rows, LANES), 1)

    for t in range(NEWTON):
        xbuf[t, 0, :, 0:width] = current
        own_logits = flat(fold(dot_t(halves(current), a_ref[...])))
        xbuf[t, 0, 0:1, width:] = own_logits
        xbuf[t, 0, 1:2, width:] = labels
        if t == 0:
            pl.semaphore_wait(barrier, nd - 1 + nz - 1)
        copies = send_all(
            "dom", xbuf.at[t, 0], lambda k: xbuf.at[t, k], lambda k: x_send.at[t, k], lambda k: x_recv.at[t, k]
        )
        pending += copies
        if t == 0:
            a_copies = send_all(
                "dom", a_ref, lambda k: basis.at[pl.ds(k * draws, draws), :],
                lambda k: a_send.at[k], lambda k: a_recv.at[k],
            )
            pending += a_copies
            spread_col = lax.broadcasted_iota(jnp.int32, spread.shape, 1) // per_row
            spread_row = lax.broadcasted_iota(jnp.int32, spread.shape, 0)
            spread[...] = (spread_col == spread_row).astype(f32).astype(bf16)
        for copy in copies:
            copy.wait_recv()
        everyone = xbuf[t, :, :, 0:width].reshape(count, width)
        pieces = halves(everyone)
        basis[cols:, :] = pieces
        for k in range(nd):
            lgt[t, 0, k : k + 1, :] = xbuf[t, k, 0:1, width:]
        inner = fold(dot_t(halves(current), pieces))
        inner = inner[:, :count] + inner[:, count:]
        sq_all = dot_t(jnp.ones((rows, width), bf16), halves(everyone * everyone))
        sq_all = sq_all[:, :count] + sq_all[:, count:]
        sq_own = jnp.sum(current * current, axis=1, keepdims=True)
        dist[t, 0, :, 0:count] = sq_own + sq_all - 2.0 * inner
        if wide > count:
            dist[t, 0, :, count:] = jnp.zeros((rows, wide - count), f32)
        c1 = send_all("dim", dist.at[t, 0], lambda k: dist.at[t, k], lambda k: d_send.at[t, k], lambda k: d_recv.at[t, k])
        c2 = send_all("dim", lgt.at[t, 0], lambda k: lgt.at[t, k], lambda k: l_send.at[t, k], lambda k: l_recv.at[t, k])
        pending += c1 + c2
        for copy in c1 + c2:
            copy.wait_recv()
        distance = functools.reduce(jnp.add, [dist[t, k] for k in range(nz)])
        logits = functools.reduce(jnp.add, [lgt[t, k] for k in range(nz)])
        prob = 1.0 / (1.0 + jnp.exp(-logits))
        curve = like_weight * prob * (1.0 - prob)
        real = first_eight < count
        kernel = jnp.where(real, jnp.exp(-distance / scale), 0.0)
        kernel_sq = kernel * kernel
        total = jnp.sum(kernel, axis=1, keepdims=True)
        total_sq = jnp.sum(kernel_sq, axis=1, keepdims=True)
        both = jnp.concatenate([kernel, kernel_sq], axis=0)[:, :count]
        wider = fold(dot(halves(both), spread[...]))
        kernel_wide, kernel_sq_wide = wider[:rows], wider[rows:]
        weight, drive = [], []
        for k in range(nd):
            part = slice(k * draws, (k + 1) * draws)
            gap = like_weight * (xbuf[t, k, 1:2, width:] - prob[k : k + 1])
            drive.append(kernel_wide[:, part] * gap)
            weight.append(kernel_sq_wide[:, part] * curve[k : k + 1])
        weight = jnp.concatenate(weight, axis=1)
        drive = jnp.concatenate(drive, axis=1)
        if t == 0:
            for copy in a_copies:
                copy.wait_recv()
        pull = (-prior_precision - 2.0 / scale) * kernel[:, :count]

        def back(on_rows, on_x):
            return fold(dot(halves(jnp.concatenate([on_rows, on_x, on_x], axis=1)), basis[...]))

        def ahead(vectors, slot):
            out = fold(dot_t(halves(vectors), basis[...]))
            proj[t, slot, 0, :, 0:cols] = out[:, :cols]
            proj[t, slot, 0, :, cols : cols + count] = out[:, cols : cols + count] + out[:, cols + count :]
            if wide > count:
                proj[t, slot, 0, :, cols + count : cols + wide] = jnp.zeros((rows, wide - count), f32)

        def exchange(slot):
            done = send_all(
                "dim", proj.at[t, slot, 0], lambda k: proj.at[t, slot, k],
                lambda k: p_send.at[t, slot, k], lambda k: p_recv.at[t, slot, k],
            )
            for copy in done:
                copy.wait_recv()
            return done, functools.reduce(jnp.add, [proj[t, slot, k] for k in range(nz)])

        def own_dots(along):
            return jnp.sum(jnp.where(own_pair, along, 0.0), axis=1, keepdims=True)

        drift = (back(drive, pull) + (2.0 / scale) * total * current) / count
        ahead(drift, 0)
        proj[t, 0, 0, :, cols + wide :] = jnp.zeros((rows, LANES), f32)
        done, seen = exchange(0)
        pending += done
        along = seen[:, cols : cols + wide]
        on_x = cross * kernel_sq * (along - own_dots(along))
        image = back(weight * seen[:, :cols], on_x[:, :count])
        image = image + prior_precision * total_sq * drift - jnp.sum(on_x, axis=1, keepdims=True) * current
        image = image / count
        ahead(image, 1)
        image_sq = jnp.sum(image * image, axis=1, keepdims=True)
        marks = jnp.where(lane == 0, jnp.sum(drift * drift, axis=1, keepdims=True), 0.0)
        marks = jnp.where(lane == 1, jnp.sum(drift * image, axis=1, keepdims=True), marks)
        marks = jnp.where(lane == 2, image_sq, marks)
        marks = jnp.where(lane == 3, prior_precision * total_sq * image_sq, marks)
        proj[t, 1, 0, :, cols + wide :] = marks
        done, seen = exchange(1)
        pending += done
        along = seen[:, cols : cols + wide]
        gap = along - own_dots(along)
        bent = jnp.sum(weight * seen[:, :cols] * seen[:, :cols], axis=1, keepdims=True)
        bent = bent + cross * jnp.sum(kernel_sq * gap * gap, axis=1, keepdims=True)
        marks = seen[:, cols + wide :]
        sums[t, 0] = marks + jnp.where(lane == 3, bent, 0.0)
        copies = send_all(
            "dom", sums.at[t, 0], lambda k: sums.at[t, k], lambda k: s_send.at[t, k], lambda k: s_recv.at[t, k]
        )
        pending += copies
        for copy in copies:
            copy.wait_recv()
        marks = functools.reduce(jnp.add, [sums[t, k] for k in range(nd)])
        marks = jnp.sum(marks, axis=0, keepdims=True)
        first = lax.broadcasted_iota(jnp.int32, (1, LANES), 1)
        norm, curve_total, image_square, bent = [
            jnp.sum(jnp.where(first == k, marks, 0.0), axis=1, keepdims=True) for k in range(4)
        ]
        bent = bent / count
        alpha = norm / curve_total
        norm_next = norm - 2.0 * alpha * curve_total + alpha * alpha * image_square
        keep = 1.0 + norm_next / norm
        curve_next = keep * keep * curve_total - 2.0 * keep * alpha * image_square + alpha * alpha * bent
        alpha_next = norm_next / curve_next
        update = (alpha + alpha_next * keep) * drift - (alpha_next * alpha) * image
        out_ref[t] = update
        current = current + move_size * update
    for copy in pending:
        copy.wait_send()


def solution(mesh):
    nd, nz = mesh.shape["dom"], mesh.shape["dim"]

    def per_device(particles, data_rows, labels):
        rows, width = particles.shape
        draws = data_rows.shape[0] * data_rows.shape[1]
        count = nd * rows
        wide = -(-count // LANES) * LANES
        cols = nd * draws
        dma = pltpu.SemaphoreType.DMA
        pairs = [(nd,), (NEWTON, nd), (NEWTON, nz), (NEWTON, nz), (NEWTON, 2, nz), (NEWTON, nd)]
        return pl.pallas_call(
            functools.partial(steps, nd, nz),
            out_shape=jax.ShapeDtypeStruct((NEWTON, rows, width), f32),
            in_specs=[pl.BlockSpec(memory_space=pltpu.VMEM)] * 3,
            out_specs=pl.BlockSpec(memory_space=pltpu.VMEM),
            scratch_shapes=[
                pltpu.VMEM((cols + 2 * count, width), bf16),
                pltpu.VMEM((count, cols), bf16),
                pltpu.VMEM((NEWTON, nd, rows, width + draws), f32),
                pltpu.VMEM((NEWTON, nz, rows, wide), f32),
                pltpu.VMEM((NEWTON, nz, nd, draws), f32),
                pltpu.VMEM((NEWTON, 2, nz, rows, cols + wide + LANES), f32),
                pltpu.VMEM((NEWTON, nd, rows, LANES), f32),
            ]
            + [dma(shape) for shape in pairs for _ in range(2)],
            compiler_params=pltpu.CompilerParams(collective_id=0, has_side_effects=True),
        )(particles, data_rows.reshape(draws, width), labels)

    placed = (P("dom", "dim"), P("dom", None, "dim"), P("dom", None))
    return jax.shard_map(
        per_device, mesh=mesh, in_specs=placed, out_specs=P(None, "dom", "dim"), check_vma=False
    )
```

time: 492 us -> 54.8 us (0.11)
  blocking collectives: 298 us -> 0 us
  waiting for transfers between devices: 126 us -> 0 us
  Pallas kernels: 0 us -> 53.2 us
  between operations: 22.8 us -> 0.01 us
  matrix products: 21.8 us -> 0 us
  other arithmetic: 9.23 us -> 0 us
  starting transfers between devices: 6.56 us -> 0 us
    psum x4 -> x0, blocking collectives: 154 us -> none  [the longest x2 77.3 us: residual_sum(): return lax.psum(jnp.sum(vectors * vectors), ('dom', 'dim'))]
    all_gather x13 -> x0, blocking collectives: 143 us -> none  [the longest x4 52.9 us: per_device(): vectors_full = lax.all_gather(direction, 'dim', axis=1, tiled=True)]
    reduce_scatter x4 -> x0, waiting for transfers between devices: 76 us -> none  [per_device(): pairs = lax.psum_scatter(pairs, 'dim', scatter_dimension=1, tiled=True)]
    pallas_call x0 -> x1, Pallas kernels: none -> 53.2 us  [per_device(): pl.pallas_call(functools.partial(steps, nd, nz), out_shape=jax.ShapeDtype...]
    psum x2 -> x0, waiting for transfers between devices: 49.8 us -> none  [per_device(): lax.psum((kernel_grad, kernel_pos, square_pos, kernel_total, square_total...]
    dot_general x28 -> x0, matrix products: 21.8 us -> none  [the longest x4 7.81 us: pair_block(): jnp.einsum('jrd,id->jri', factor_part, vectors, precision=highest)]
    reduce_sum x12 -> x0, other arithmetic: 6.76 us -> none  [the longest x2 2.93 us: per_device(): jnp.sum(image * image)]
    all_to_all x1 -> x0, starting transfers between devices: 6.35 us -> none  [per_device(): lax.all_to_all(data_rows, 'dim', split_axis=0, concat_axis=2, tiled=True)]
  transfers between devices with their start and end apart: 7 -> 0, of which waited for: 6 -> 0; matrix products, arithmetic and copies ran while one was open for 0% -> 0% of each run, Pallas kernels for 0% -> 0%
where the time goes in v1:
time: 54.8 us; the launch traced here: 54.6 us
  Pallas kernels  53.2 us (97%)
  local copies, waits for them, and re-layouts  1.32 us (2%)
    pallas_call x1, Pallas kernels, per_device(): pl.pallas_call(functools.partial(steps, nd, nz), out_shape=jax.ShapeDtype...  53.2 us
    unnamed x1, local copies, waits for them, and re-layouts  1.32 us

profile of v1, /device:TPU:0, one launch (start us, length us, event | category | flops | bytes accessed | tf_op | source)
XLA Modules:
  0.0 54.6 jit_solution(5288369139058621748)
XLA Ops:
  0.0 53.2 %shard_map.37 = f32[2,8,256]{2,1,0:T(8,128)} custom-call(f32[8,256]{1,0:T(8,128)} %x_ref.1, bf16[128,256]{1,0:T(8,128)(2,1)} %bitcast.1, s32[8,16]{1,0:T(8,128)} %y_ref.1), custom_call_target="tpu_custom_call" | custom-call | tf_op jit(solution)/shard_map/pallas_call | solution.py:242
  53.2 1.3 %copy.5 = f32[2,8,256]{2,1,0:T(8,128)} copy(f32[2,8,256]{2,1,0:T(8,128)} %shard_map.37) | data formatting | bytes 32768

commit v2 on v1

--- a/solution.py
+++ b/solution.py
@@ -39,8 +39,9 @@
 
 def steps(
     nd, nz, x_ref, a_ref, y_ref, out_ref,
-    basis, spread, xbuf, dist, lgt, proj, sums,
-    a_send, a_recv, x_send, x_recv, d_send, d_recv, l_send, l_recv, p_send, p_recv, s_send, s_recv,
+    basis, spread, xbuf, dist, lgt, proj, rough, marked, sums,
+    a_send, a_recv, x_send, x_recv, d_send, d_recv, l_send, l_recv, p_send, p_recv,
+    r_send, r_recv, m_send, m_recv, s_send, s_recv,
 ):
     rows, width = x_ref.shape
     draws = a_ref.shape[0]
@@ -52,26 +53,39 @@
     cross = 4.0 / (scale * scale)
     me_dom = lax.axis_index("dom")
     me_dim = lax.axis_index("dim")
-    dom_to = [None] + [lax.rem(me_dom + k, nd) for k in range(1, nd)]
-    dim_to = [None] + [lax.rem(me_dim + k, nz) for k in range(1, nz)]
-
-    def send_all(axis, src, dst, send, recv):
-        to = dom_to if axis == "dom" else dim_to
-        copies = []
-        for k in range(1, len(to)):
-            copy = pltpu.make_async_remote_copy(
+    chips = nd // 2
+    chip, core = me_dom // 2, me_dom % 2
+    dom_to = [((chip + m // 2) % chips) * 2 + (core + m) % 2 for m in range(nd)]
+    upper = (me_dim * 2) // nz
+
+    def dom_copy(m, src, dst, send, recv):
+        return pltpu.make_async_remote_copy(
+            src_ref=src, dst_ref=dst(m), send_sem=send(m), recv_sem=recv(m),
+            device_id={"dom": dom_to[m]}, device_id_type=MESH,
+        )
+
+    def send_dom(*what):
+        copies = [dom_copy(m, *what) for m in range(1, nd)]
+        for copy in copies:
+            copy.start()
+        return copies
+
+    def send_dim(src, dst, send, recv):
+        def one(k):
+            return pltpu.make_async_remote_copy(
                 src_ref=src, dst_ref=dst(k), send_sem=send(k), recv_sem=recv(k),
-                device_id={axis: to[k]}, device_id_type=MESH,
+                device_id={"dim": lax.rem(me_dim + k, nz)}, device_id_type=MESH,
             )
-            copy.start()
-            copies.append(copy)
-        return copies
+
+        for k in range(1, nz):
+            one(upper * k + (1 - upper) * (nz - k)).start()
+        return [one(k) for k in range(1, nz)]
 
     barrier = pltpu.get_barrier_semaphore()
     for k in range(1, nd):
         pl.semaphore_signal(barrier, inc=1, device_id={"dom": dom_to[k]}, device_id_type=MESH)
     for k in range(1, nz):
-        pl.semaphore_signal(barrier, inc=1, device_id={"dim": dim_to[k]}, device_id_type=MESH)
+        pl.semaphore_signal(barrier, inc=1, device_id={"dim": lax.rem(me_dim + k, nz)}, device_id_type=MESH)
 
     lane_of = lax.broadcasted_iota(jnp.int32, (rows, draws), 1) // per_row
     row_of = lax.broadcasted_iota(jnp.int32, (rows, draws), 0)
@@ -86,7 +100,6 @@
     labels = flat(dot(y_ref[...].astype(f32).astype(bf16), tile))
     current = x_ref[...]
     pending = []
-    a_copies = []
     first_eight = lax.broadcasted_iota(jnp.int32, (rows, wide), 1)
     own_pair = first_eight == lax.broadcasted_iota(jnp.int32, (rows, wide), 0)
     lane = lax.broadcasted_iota(jnp.int32, (rows, LANES), 1)
@@ -98,16 +111,18 @@
         xbuf[t, 0, 1:2, width:] = labels
         if t == 0:
             pl.semaphore_wait(barrier, nd - 1 + nz - 1)
-        copies = send_all(
-            "dom", xbuf.at[t, 0], lambda k: xbuf.at[t, k], lambda k: x_send.at[t, k], lambda k: x_recv.at[t, k]
+        copies = send_dom(
+            xbuf.at[t, 0], lambda k: xbuf.at[t, k], lambda k: x_send.at[t, k], lambda k: x_recv.at[t, k]
         )
         pending += copies
         if t == 0:
-            a_copies = send_all(
-                "dom", a_ref, lambda k: basis.at[pl.ds(k * draws, draws), :],
-                lambda k: a_send.at[k], lambda k: a_recv.at[k],
+            a_parts = (
+                lambda k: basis.at[pl.ds(k * draws, draws), :], lambda k: a_send.at[k], lambda k: a_recv.at[k],
             )
-            pending += a_copies
+            a_far = [dom_copy(m, a_ref, *a_parts) for m in range(2, nd, 2)]
+            a_near = [dom_copy(1, a_ref, *a_parts)]
+            for copy in a_far + a_near:
+                copy.start()
             spread_col = lax.broadcasted_iota(jnp.int32, spread.shape, 1) // per_row
             spread_row = lax.broadcasted_iota(jnp.int32, spread.shape, 0)
             spread[...] = (spread_col == spread_row).astype(f32).astype(bf16)
@@ -126,9 +141,21 @@
         dist[t, 0, :, 0:count] = sq_own + sq_all - 2.0 * inner
         if wide > count:
             dist[t, 0, :, count:] = jnp.zeros((rows, wide - count), f32)
-        c1 = send_all("dim", dist.at[t, 0], lambda k: dist.at[t, k], lambda k: d_send.at[t, k], lambda k: d_recv.at[t, k])
-        c2 = send_all("dim", lgt.at[t, 0], lambda k: lgt.at[t, k], lambda k: l_send.at[t, k], lambda k: l_recv.at[t, k])
+        c1 = send_dim(dist.at[t, 0], lambda k: dist.at[t, k], lambda k: d_send.at[t, k], lambda k: d_recv.at[t, k])
+        c2 = send_dim(lgt.at[t, 0], lambda k: lgt.at[t, k], lambda k: l_send.at[t, k], lambda k: l_recv.at[t, k])
         pending += c1 + c2
+        if t == 0:
+            for m, copy in zip(range(2, nd, 2), a_far):
+                copy.wait_recv()
+                part = basis.at[pl.ds(m * draws, draws), :]
+                on = pltpu.make_async_remote_copy(
+                    src_ref=part, dst_ref=basis.at[pl.ds((m + 1) * draws, draws), :],
+                    send_sem=a_send.at[m + 1], recv_sem=a_recv.at[m + 1],
+                    device_id={"dom": dom_to[1]}, device_id_type=MESH,
+                )
+                on.start()
+                a_near.append(on)
+            pending += a_far + a_near
         for copy in c1 + c2:
             copy.wait_recv()
         distance = functools.reduce(jnp.add, [dist[t, k] for k in range(nz)])
@@ -152,59 +179,57 @@
         weight = jnp.concatenate(weight, axis=1)
         drive = jnp.concatenate(drive, axis=1)
         if t == 0:
-            for copy in a_copies:
+            for copy in a_near:
                 copy.wait_recv()
         pull = (-prior_precision - 2.0 / scale) * kernel[:, :count]
 
         def back(on_rows, on_x):
             return fold(dot(halves(jnp.concatenate([on_rows, on_x, on_x], axis=1)), basis[...]))
 
-        def ahead(vectors, slot):
+        def ahead(vectors):
             out = fold(dot_t(halves(vectors), basis[...]))
-            proj[t, slot, 0, :, 0:cols] = out[:, :cols]
-            proj[t, slot, 0, :, cols : cols + count] = out[:, cols : cols + count] + out[:, cols + count :]
+            parts = [out[:, :cols], out[:, cols : cols + count] + out[:, cols + count :]]
             if wide > count:
-                proj[t, slot, 0, :, cols + count : cols + wide] = jnp.zeros((rows, wide - count), f32)
-
-        def exchange(slot):
-            done = send_all(
-                "dim", proj.at[t, slot, 0], lambda k: proj.at[t, slot, k],
-                lambda k: p_send.at[t, slot, k], lambda k: p_recv.at[t, slot, k],
-            )
-            for copy in done:
-                copy.wait_recv()
-            return done, functools.reduce(jnp.add, [proj[t, slot, k] for k in range(nz)])
+                parts.append(jnp.zeros((rows, wide - count), f32))
+            return jnp.concatenate(parts, axis=1)
 
         def own_dots(along):
             return jnp.sum(jnp.where(own_pair, along, 0.0), axis=1, keepdims=True)
 
         drift = (back(drive, pull) + (2.0 / scale) * total * current) / count
-        ahead(drift, 0)
-        proj[t, 0, 0, :, cols + wide :] = jnp.zeros((rows, LANES), f32)
-        done, seen = exchange(0)
-        pending += done
+        proj[t, 0] = ahead(drift)
+        copies = send_dim(proj.at[t, 0], lambda k: proj.at[t, k], lambda k: p_send.at[t, k], lambda k: p_recv.at[t, k])
+        pending += copies
+        for copy in copies:
+            copy.wait_recv()
+        seen = functools.reduce(jnp.add, [proj[t, k] for k in range(nz)])
         along = seen[:, cols : cols + wide]
         on_x = cross * kernel_sq * (along - own_dots(along))
         image = back(weight * seen[:, :cols], on_x[:, :count])
         image = image + prior_precision * total_sq * drift - jnp.sum(on_x, axis=1, keepdims=True) * current
         image = image / count
-        ahead(image, 1)
+        exact = ahead(image)
+        rough[t, 0] = exact.astype(bf16)
+        c1 = send_dim(rough.at[t, 0], lambda k: rough.at[t, k], lambda k: r_send.at[t, k], lambda k: r_recv.at[t, k])
         image_sq = jnp.sum(image * image, axis=1, keepdims=True)
         marks = jnp.where(lane == 0, jnp.sum(drift * drift, axis=1, keepdims=True), 0.0)
         marks = jnp.where(lane == 1, jnp.sum(drift * image, axis=1, keepdims=True), marks)
         marks = jnp.where(lane == 2, image_sq, marks)
         marks = jnp.where(lane == 3, prior_precision * total_sq * image_sq, marks)
-        proj[t, 1, 0, :, cols + wide :] = marks
-        done, seen = exchange(1)
-        pending += done
+        marked[t, 0] = marks
+        c2 = send_dim(marked.at[t, 0], lambda k: marked.at[t, k], lambda k: m_send.at[t, k], lambda k: m_recv.at[t, k])
+        pending += c1 + c2
+        for copy in c1 + c2:
+            copy.wait_recv()
+        seen = functools.reduce(jnp.add, [rough[t, k].astype(f32) for k in range(1, nz)], exact)
         along = seen[:, cols : cols + wide]
         gap = along - own_dots(along)
         bent = jnp.sum(weight * seen[:, :cols] * seen[:, :cols], axis=1, keepdims=True)
         bent = bent + cross * jnp.sum(kernel_sq * gap * gap, axis=1, keepdims=True)
-        marks = seen[:, cols + wide :]
+        marks = functools.reduce(jnp.add, [marked[t, k] for k in range(nz)])
         sums[t, 0] = marks + jnp.where(lane == 3, bent, 0.0)
-        copies = send_all(
-            "dom", sums.at[t, 0], lambda k: sums.at[t, k], lambda k: s_send.at[t, k], lambda k: s_recv.at[t, k]
+        copies = send_dom(
+            sums.at[t, 0], lambda k: sums.at[t, k], lambda k: s_send.at[t, k], lambda k: s_recv.at[t, k]
         )
         pending += copies
         for copy in copies:
@@ -238,7 +263,8 @@
         wide = -(-count // LANES) * LANES
         cols = nd * draws
         dma = pltpu.SemaphoreType.DMA
-        pairs = [(nd,), (NEWTON, nd), (NEWTON, nz), (NEWTON, nz), (NEWTON, 2, nz), (NEWTON, nd)]
+        over_dom, over_dim = (NEWTON, nd), (NEWTON, nz)
+        pairs = [(nd,), over_dom] + [over_dim] * 5 + [over_dom]
         return pl.pallas_call(
             functools.partial(steps, nd, nz),
             out_shape=jax.ShapeDtypeStruct((NEWTON, rows, width), f32),
@@ -250,7 +276,9 @@
                 pltpu.VMEM((NEWTON, nd, rows, width + draws), f32),
                 pltpu.VMEM((NEWTON, nz, rows, wide), f32),
                 pltpu.VMEM((NEWTON, nz, nd, draws), f32),
-                pltpu.VMEM((NEWTON, 2, nz, rows, cols + wide + LANES), f32),
+                pltpu.VMEM((NEWTON, nz, rows, cols + wide), f32),
+                pltpu.VMEM((NEWTON, nz, rows, cols + wide), bf16),
+                pltpu.VMEM((NEWTON, nz, rows, LANES), f32),
                 pltpu.VMEM((NEWTON, nd, rows, LANES), f32),
             ]
             + [dma(shape) for shape in pairs for _ in range(2)],

time: 54.8 us -> 50.7 us (0.925)
  Pallas kernels: 53.2 us -> 49.1 us
    pallas_call x1, Pallas kernels: 53.2 us -> 49.1 us  [per_device(): pl.pallas_call(functools.partial(steps, nd, nz), out_shape=jax.ShapeDtype...]
where the time goes in v2:
time: 50.7 us; the launch traced here: 50.4 us
  Pallas kernels  49.1 us (97%)
  local copies, waits for them, and re-layouts  1.32 us (3%)
    pallas_call x1, Pallas kernels, per_device(): pl.pallas_call(functools.partial(steps, nd, nz), out_shape=jax.ShapeDtype...  49.1 us
    unnamed x1, local copies, waits for them, and re-layouts  1.32 us

profile of v2, /device:TPU:0, one launch (start us, length us, event | category | flops | bytes accessed | tf_op | source)
XLA Modules:
  0.0 50.4 jit_solution(638059118344824526)
XLA Ops:
  0.0 49.1 %shard_map.37 = f32[2,8,256]{2,1,0:T(8,128)} custom-call(f32[8,256]{1,0:T(8,128)} %x_ref.1, bf16[128,256]{1,0:T(8,128)(2,1)} %bitcast.1, s32[8,16]{1,0:T(8,128)} %y_ref.1), custom_call_target="tpu_custom_call" | custom-call | tf_op jit(solution)/shard_map/pallas_call | solution.py:268
  49.1 1.3 %copy.5 = f32[2,8,256]{2,1,0:T(8,128)} copy(f32[2,8,256]{2,1,0:T(8,128)} %shard_map.37) | data formatting | bytes 32768

commit v3 on v2

v3 whole, which is shorter than its diff:
```python
import functools

import jax
import jax.numpy as jnp
from jax import lax
from jax.experimental import pallas as pl
from jax.experimental.pallas import tpu as pltpu
from jax.sharding import PartitionSpec as P

NEWTON = 2
BAND = 1
LANES = 128

prior_precision = 0.05
like_weight = 4.0
move_size = 0.5
MESH = pl.DeviceIdType.MESH
f32 = jnp.float32
bf16 = jnp.bfloat16


def halves(v):
    high = v.astype(bf16).astype(f32)
    return jnp.concatenate([high, v - high], axis=0).astype(bf16)


def fold(product):
    rows = product.shape[0] // 2
    return product[:rows] + product[rows:]


def dot(a, b):
    return lax.dot_general(a, b, (((1,), (0,)), ((), ())), preferred_element_type=f32)


def dot_t(a, b):
    return lax.dot_general(a, b, (((1,), (1,)), ((), ())), preferred_element_type=f32)


def steps(
    nd, nz, x_ref, a_ref, y_ref, out_ref,
    basis, spread, xbuf, dist, lgt, proj, rough, marked, sums, moves, cross_terms,
    a_send, a_recv, x_send, x_recv, d_send, d_recv, l_send, l_recv, p_send, p_recv,
    r_send, r_recv, m_send, m_recv, s_send, s_recv,
    b_send, b_recv, h_send, h_recv, g_send, g_recv,
):
    rows, width = x_ref.shape
    draws = a_ref.shape[0]
    per_row = draws // rows
    count = nd * rows
    wide = dist.shape[-1]
    cols = nd * draws
    scale = 1.0 * BAND * width * nz
    cross = 4.0 / (scale * scale)
    me_dom = lax.axis_index("dom")
    me_dim = lax.axis_index("dim")
    chips = nd // 2
    chip, core = me_dom // 2, me_dom % 2
    dom_to = [((chip + m // 2) % chips) * 2 + (core + m) % 2 for m in range(nd)]
    upper = (me_dim * 2) // nz

    def dom_copy(m, src, dst, send, recv):
        return pltpu.make_async_remote_copy(
            src_ref=src, dst_ref=dst(m), send_sem=send(m), recv_sem=recv(m),
            device_id={"dom": dom_to[m]}, device_id_type=MESH,
        )

    def send_dom(*what):
        copies = [dom_copy(m, *what) for m in range(1, nd)]
        for copy in copies:
            copy.start()
        return copies

    def send_dim(src, dst, send, recv):
        def one(k):
            return pltpu.make_async_remote_copy(
                src_ref=src, dst_ref=dst(k), send_sem=send(k), recv_sem=recv(k),
                device_id={"dim": lax.rem(me_dim + k, nz)}, device_id_type=MESH,
            )

        for k in range(1, nz):
            one(upper * k + (1 - upper) * (nz - k)).start()
        return [one(k) for k in range(1, nz)]

    barrier = pltpu.get_barrier_semaphore()
    for k in range(1, nd):
        pl.semaphore_signal(barrier, inc=1, device_id={"dom": dom_to[k]}, device_id_type=MESH)
    for k in range(1, nz):
        pl.semaphore_signal(barrier, inc=1, device_id={"dim": lax.rem(me_dim + k, nz)}, device_id_type=MESH)

    lane_of = lax.broadcasted_iota(jnp.int32, (rows, draws), 1) // per_row
    row_of = lax.broadcasted_iota(jnp.int32, (rows, draws), 0)
    own_block = lane_of == row_of

    def flat(values):
        return jnp.sum(jnp.where(own_block, values, 0.0), axis=0, keepdims=True)

    basis[0:draws, :] = a_ref[...]
    tile = lax.broadcasted_iota(jnp.int32, (per_row, draws), 1) % per_row
    tile = (tile == lax.broadcasted_iota(jnp.int32, (per_row, draws), 0)).astype(f32).astype(bf16)
    labels = flat(dot(y_ref[...].astype(f32).astype(bf16), tile))
    current = x_ref[...]
    pending = []
    first_eight = lax.broadcasted_iota(jnp.int32, (rows, count), 1)
    own_pair = first_eight == lax.broadcasted_iota(jnp.int32, (rows, count), 0)
    lane = lax.broadcasted_iota(jnp.int32, (rows, LANES), 1)

    def paired(product):
        return product[:, : product.shape[1] // 2] + product[:, product.shape[1] // 2 :]

    def column_sums(values):
        return paired(dot_t(jnp.ones((rows, width), bf16), halves(values)))

    def row_sums(values):
        return jnp.sum(values, axis=1, keepdims=True)

    xbuf[0, :, 0:width] = current
    xbuf[0, 0:1, width:] = flat(fold(dot_t(halves(current), a_ref[...])))
    xbuf[0, 1:2, width:] = labels
    pl.semaphore_wait(barrier, nd - 1 + nz - 1)
    copies = send_dom(xbuf.at[0], lambda k: xbuf.at[k], lambda k: x_send.at[k], lambda k: x_recv.at[k])
    pending += copies
    a_parts = (
        lambda k: basis.at[pl.ds(k * draws, draws), :], lambda k: a_send.at[k], lambda k: a_recv.at[k],
    )
    a_far = [dom_copy(m, a_ref, *a_parts) for m in range(2, nd, 2)]
    a_near = [dom_copy(1, a_ref, *a_parts)]
    for copy in a_far + a_near:
        copy.start()
    spread_col = lax.broadcasted_iota(jnp.int32, spread.shape, 1) // per_row
    spread_row = lax.broadcasted_iota(jnp.int32, spread.shape, 0)
    spread[...] = (spread_col == spread_row).astype(f32).astype(bf16)
    for copy in copies:
        copy.wait_recv()
    everyone = xbuf[:, :, 0:width].reshape(count, width)
    pieces = halves(everyone)
    basis[cols:, :] = pieces
    for k in range(nd):
        lgt[0, k : k + 1, :] = xbuf[k, 0:1, width:]
    inner = paired(fold(dot_t(halves(current), pieces)))
    dist[0, :, 0:count] = row_sums(current * current) + column_sums(everyone * everyone) - 2.0 * inner
    if wide > count:
        dist[0, :, count:] = jnp.zeros((rows, wide - count), f32)
    c1 = send_dim(dist.at[0], lambda k: dist.at[k], lambda k: d_send.at[k], lambda k: d_recv.at[k])
    c2 = send_dim(lgt.at[0], lambda k: lgt.at[k], lambda k: l_send.at[k], lambda k: l_recv.at[k])
    pending += c1 + c2
    for m, copy in zip(range(2, nd, 2), a_far):
        copy.wait_recv()
        on = pltpu.make_async_remote_copy(
            src_ref=basis.at[pl.ds(m * draws, draws), :], dst_ref=basis.at[pl.ds((m + 1) * draws, draws), :],
            send_sem=a_send.at[m + 1], recv_sem=a_recv.at[m + 1],
            device_id={"dom": dom_to[1]}, device_id_type=MESH,
        )
        on.start()
        a_near.append(on)
    pending += a_far + a_near
    for copy in c1 + c2:
        copy.wait_recv()
    distance = functools.reduce(jnp.add, [dist[k] for k in range(nz)])[:, :count]
    logits = functools.reduce(jnp.add, [lgt[k] for k in range(nz)])

    for t in range(NEWTON):
        last = t + 1 == NEWTON
        prob = 1.0 / (1.0 + jnp.exp(-logits))
        curve = like_weight * prob * (1.0 - prob)
        kernel = jnp.exp(-distance / scale)
        kernel_sq = kernel * kernel
        total = jnp.sum(kernel, axis=1, keepdims=True)
        total_sq = jnp.sum(kernel_sq, axis=1, keepdims=True)
        both = jnp.concatenate([kernel, kernel_sq], axis=0)
        wider = fold(dot(halves(both), spread[...]))
        kernel_wide, kernel_sq_wide = wider[:rows], wider[rows:]
        weight, drive = [], []
        for k in range(nd):
            part = slice(k * draws, (k + 1) * draws)
            gap = like_weight * (xbuf[k, 1:2, width:] - prob[k : k + 1])
            drive.append(kernel_wide[:, part] * gap)
            weight.append(kernel_sq_wide[:, part] * curve[k : k + 1])
        weight = jnp.concatenate(weight, axis=1)
        drive = jnp.concatenate(drive, axis=1)
        if t == 0:
            for copy in a_near:
                copy.wait_recv()
        pull = (-prior_precision - 2.0 / scale) * kernel

        def back(on_rows, on_x):
            return fold(dot(halves(jnp.concatenate([on_rows, on_x, on_x], axis=1)), basis[...]))

        def ahead(vectors):
            out = fold(dot_t(halves(vectors), basis[...]))
            parts = [out[:, :cols], out[:, cols : cols + count] + out[:, cols + count :]]
            if wide > count:
                parts.append(jnp.zeros((rows, wide - count), f32))
            return jnp.concatenate(parts, axis=1)

        def own_dots(along):
            return jnp.sum(jnp.where(own_pair, along, 0.0), axis=1, keepdims=True)

        drift = (back(drive, pull) + (2.0 / scale) * total * current) / count
        proj[t, 0] = ahead(drift)
        copies = send_dim(proj.at[t, 0], lambda k: proj.at[t, k], lambda k: p_send.at[t, k], lambda k: p_recv.at[t, k])
        pending += copies
        if not last:
            moves[t, 0, 0] = drift
            b_copies = send_dom(
                moves.at[t, 0, 0], lambda k: moves.at[t, 0, k], lambda k: b_send.at[t, k], lambda k: b_recv.at[t, k]
            )
            pending += b_copies
        for copy in copies:
            copy.wait_recv()
        seen = functools.reduce(jnp.add, [proj[t, k] for k in range(nz)])
        drift_logits = flat(seen[:, :draws])
        along = seen[:, cols : cols + count]
        on_x = cross * kernel_sq * (along - own_dots(along))
        image = back(weight * seen[:, :cols], on_x)
        image = image + prior_precision * total_sq * drift - jnp.sum(on_x, axis=1, keepdims=True) * current
        image = image / count
        if not last:
            moves[t, 1, 0] = image
            h_copies = send_dom(
                moves.at[t, 1, 0], lambda k: moves.at[t, 1, k], lambda k: h_send.at[t, k], lambda k: h_recv.at[t, k]
            )
            pending += h_copies
        exact = ahead(image)
        rough[t, 0] = exact.astype(bf16)
        c1 = send_dim(rough.at[t, 0], lambda k: rough.at[t, k], lambda k: r_send.at[t, k], lambda k: r_recv.at[t, k])
        image_sq = jnp.sum(image * image, axis=1, keepdims=True)
        marks = jnp.where(lane == 0, jnp.sum(drift * drift, axis=1, keepdims=True), 0.0)
        marks = jnp.where(lane == 1, jnp.sum(drift * image, axis=1, keepdims=True), marks)
        marks = jnp.where(lane == 2, image_sq, marks)
        marks = jnp.where(lane == 3, prior_precision * total_sq * image_sq, marks)
        marked[t, 0] = jnp.concatenate(
            [jnp.sum(marks, axis=0, keepdims=True), flat(exact[:, :draws]), jnp.zeros((rows - 2, LANES), f32)], axis=0
        )
        c2 = send_dim(marked.at[t, 0], lambda k: marked.at[t, k], lambda k: m_send.at[t, k], lambda k: m_recv.at[t, k])
        pending += c1 + c2
        if not last:
            for copy in b_copies + h_copies:
                copy.wait_recv()
            every = [everyone, moves[t, 0].reshape(count, width), moves[t, 1].reshape(count, width)]
            own = [current, drift, image]
            pairs = [(0, 1), (0, 2), (1, 1), (1, 2), (2, 2)]
            own_pieces = halves(jnp.concatenate(own, axis=0))
            inner = [paired(fold(dot_t(own_pieces, halves(v)))) for v in every]
            square = column_sums(jnp.concatenate([every[u] * every[v] for u, v in pairs], axis=0))
            terms = []
            for n, (u, v) in enumerate(pairs):
                mixed = inner[v][u * rows : (u + 1) * rows] + inner[u][v * rows : (v + 1) * rows]
                terms.append(row_sums(own[u] * own[v]) + square[:, n * count : (n + 1) * count] - mixed)
            spare = cross_terms.shape[-1] - len(pairs) * count
            if spare > 0:
                terms.append(jnp.zeros((rows, spare), f32))
            cross_terms[t, 0] = jnp.concatenate(terms, axis=1)
            g_copies = send_dim(
                cross_terms.at[t, 0], lambda k: cross_terms.at[t, k], lambda k: g_send.at[t, k], lambda k: g_recv.at[t, k]
            )
            pending += g_copies
        for copy in c1 + c2:
            copy.wait_recv()
        seen = functools.reduce(jnp.add, [rough[t, k].astype(f32) for k in range(1, nz)], exact)
        along = seen[:, cols : cols + count]
        gap = along - own_dots(along)
        bent = jnp.sum(weight * seen[:, :cols] * seen[:, :cols], axis=1, keepdims=True)
        bent = bent + cross * jnp.sum(kernel_sq * gap * gap, axis=1, keepdims=True)
        marks = functools.reduce(jnp.add, [marked[t, k] for k in range(nz)])
        bent = jnp.sum(bent, axis=0, keepdims=True)
        sums[t, 0] = jnp.concatenate(
            [marks[0:1] + jnp.where(lane[0:1] == 3, bent, 0.0), drift_logits, marks[1:2], marks[3:]], axis=0
        )
        copies = send_dom(
            sums.at[t, 0], lambda k: sums.at[t, k], lambda k: s_send.at[t, k], lambda k: s_recv.at[t, k]
        )
        pending += copies
        for copy in copies:
            copy.wait_recv()
        marks = functools.reduce(jnp.add, [sums[t, k, 0:1] for k in range(nd)])
        first = lax.broadcasted_iota(jnp.int32, (1, LANES), 1)
        norm, curve_total, image_square, bent = [
            jnp.sum(jnp.where(first == k, marks, 0.0), axis=1, keepdims=True) for k in range(4)
        ]
        bent = bent / count
        alpha = norm / curve_total
        norm_next = norm - 2.0 * alpha * curve_total + alpha * alpha * image_square
        keep = 1.0 + norm_next / norm
        curve_next = keep * keep * curve_total - 2.0 * keep * alpha * image_square + alpha * alpha * bent
        alpha_next = norm_next / curve_next
        on_drift, on_image = alpha + alpha_next * keep, -alpha_next * alpha
        update = on_drift * drift + on_image * image
        out_ref[t] = update
        if not last:
            current = current + move_size * update
            step_b, step_h = move_size * on_drift, move_size * on_image
            everyone = everyone + step_b * every[1] + step_h * every[2]
            basis[cols:, :] = halves(everyone)
            shifts = [sums[t, k, 1:2] * step_b + sums[t, k, 2:3] * step_h for k in range(nd)]
            logits = logits + jnp.concatenate(shifts, axis=0)
            for copy in g_copies:
                copy.wait_recv()
            terms = functools.reduce(jnp.add, [cross_terms[t, k] for k in range(nz)])
            by = [2.0 * step_b, 2.0 * step_h, step_b * step_b, 2.0 * step_b * step_h, step_h * step_h]
            for n, factor in enumerate(by):
                distance = distance + factor * terms[:, n * count : (n + 1) * count]
    for copy in pending:
        copy.wait_send()


def solution(mesh):
    nd, nz = mesh.shape["dom"], mesh.shape["dim"]

    def per_device(particles, data_rows, labels):
        rows, width = particles.shape
        draws = data_rows.shape[0] * data_rows.shape[1]
        count = nd * rows
        wide = -(-count // LANES) * LANES
        cols = nd * draws
        dma = pltpu.SemaphoreType.DMA
        over_dom, over_dim = (NEWTON, nd), (NEWTON, nz)
        pairs = [(nd,), (nd,), (nz,), (nz,)] + [over_dim] * 3 + [over_dom] * 3 + [over_dim]
        return pl.pallas_call(
            functools.partial(steps, nd, nz),
            out_shape=jax.ShapeDtypeStruct((NEWTON, rows, width), f32),
            in_specs=[pl.BlockSpec(memory_space=pltpu.VMEM)] * 3,
            out_specs=pl.BlockSpec(memory_space=pltpu.VMEM),
            scratch_shapes=[
                pltpu.VMEM((cols + 2 * count, width), bf16),
                pltpu.VMEM((count, cols), bf16),
                pltpu.VMEM((nd, rows, width + draws), f32),
                pltpu.VMEM((nz, rows, wide), f32),
                pltpu.VMEM((nz, nd, draws), f32),
                pltpu.VMEM((NEWTON, nz, rows, cols + wide), f32),
                pltpu.VMEM((NEWTON, nz, rows, cols + wide), bf16),
                pltpu.VMEM((NEWTON, nz, rows, LANES), f32),
                pltpu.VMEM((NEWTON, nd, rows, LANES), f32),
                pltpu.VMEM((NEWTON, 2, nd, rows, width), f32),
                pltpu.VMEM((NEWTON, nz, rows, -(-5 * count // LANES) * LANES), f32),
            ]
            + [dma(shape) for shape in pairs for _ in range(2)],
            compiler_params=pltpu.CompilerParams(collective_id=0, has_side_effects=True),
        )(particles, data_rows.reshape(draws, width), labels)

    placed = (P("dom", "dim"), P("dom", None, "dim"), P("dom", None))
    return jax.shard_map(
        per_device, mesh=mesh, in_specs=placed, out_specs=P(None, "dom", "dim"), check_vma=False
    )
```

time: 50.7 us -> 44.6 us (0.88)
  Pallas kernels: 49.1 us -> 43 us
    pallas_call x1, Pallas kernels: 49.1 us -> 43 us  [per_device(): pl.pallas_call(functools.partial(steps, nd, nz), out_shape=jax.ShapeDtype...]
where the time goes in v3:
time: 44.6 us; the launch traced here: 44.3 us
  Pallas kernels  43 us (96%)
  local copies, waits for them, and re-layouts  1.32 us (3%)
    pallas_call x1, Pallas kernels, per_device(): pl.pallas_call(functools.partial(steps, nd, nz), out_shape=jax.ShapeDtype...  43 us
    unnamed x1, local copies, waits for them, and re-layouts  1.32 us

profile of v3, /device:TPU:0, one launch (start us, length us, event | category | flops | bytes accessed | tf_op | source)
XLA Modules:
  0.0 44.3 jit_solution(1801213143807143472)
XLA Ops:
  0.0 43.0 %shard_map.37 = f32[2,8,256]{2,1,0:T(8,128)} custom-call(f32[8,256]{1,0:T(8,128)} %x_ref.1, bf16[128,256]{1,0:T(8,128)(2,1)} %bitcast.1, s32[8,16]{1,0:T(8,128)} %y_ref.1), custom_call_target="tpu_custom_call" | custom-call | tf_op jit(solution)/shard_map/pallas_call | solution.py:319
  43.0 1.3 %copy.5 = f32[2,8,256]{2,1,0:T(8,128)} copy(f32[2,8,256]{2,1,0:T(8,128)} %shard_map.37) | data formatting | bytes 32768
